TPU v7x, 32 devices: a whole 2x2x4 slice. The times are simulated.
32 devices in a mesh: path: 16 (over z, x, core), shard: 2 (over y).
Axes of the slice: x: 2, y: 2, z: 4, core: 2. Of those that a mesh axis runs over, the one named last changes fastest.
Arguments:
- deltas: bfloat16 [16, 32, 4096], P('path', 'shard'), may hold values from -96 to 96
- momentum: float32 [16, 32, 4096], P(None, 'shard', 'path'), may hold values from -4 to 4
- path_module: int32 [16], replicated, may hold values from 0 to 15, as said below
Outputs:
- path_update: bfloat16 [16, 32, 4096], P('path', 'shard')
- new_momentum: float32 [16, 32, 4096], P(None, 'shard', 'path')
Inputs may be any that keep to these rules, and one draw needn't show every extreme that they name: `path_module`: every module is used by at least one and at most seven paths.
All inputs are finite; a program needn't handle non-finite values.
Results may differ from a plain program's by a relative error of at most 0.0004.
Values may be sent and summed in bfloat16 or wider, within the bound.
A program may use at most 64 MiB of HBM per device.

v0:
```python
import jax
import jax.numpy as jnp
from jax import lax
from jax.sharding import PartitionSpec as P

D = 4096
outer_rate = 0.7
momentum_rate = 0.9
clip_ratio = 2.0


def local(deltas, momentum, path_module):
    own_index = lax.axis_index("path")
    modules = momentum.shape[0]
    row_count = deltas.shape[1]
    onehot = (path_module[:, None] == jnp.arange(modules, dtype=jnp.int32)[None, :]).astype(
        jnp.float32
    )
    counts = jnp.sum(onehot, axis=0)
    own_module = lax.dynamic_index_in_dim(path_module, own_index, 0, keepdims=False)
    column_pieces = lax.all_to_all(deltas, "path", split_axis=2, concat_axis=0, tiled=True)
    totals = jnp.einsum(
        "pm,prc->mrc",
        onehot.astype(jnp.bfloat16),
        column_pieces,
        preferred_element_type=jnp.float32,
    )
    outer_grad = totals / counts[:, None, None]
    local_squares = jnp.sum(outer_grad * outer_grad, axis=(1, 2))
    norm_squares = lax.psum(local_squares, ("path", "shard"))
    limit = clip_ratio * jnp.sqrt(jnp.float32(row_count * lax.axis_size("shard") * D))
    shrink = jnp.minimum(1.0, limit / jnp.sqrt(norm_squares + 1e-06))
    clipped = outer_grad * shrink[:, None, None]
    new_momentum = momentum_rate * momentum + clipped
    outer_step = (outer_rate * (clipped + momentum_rate * new_momentum)).astype(jnp.bfloat16)
    gathered = lax.all_gather(outer_step, "path", axis=2, tiled=True)
    path_update = lax.dynamic_index_in_dim(gathered, own_module, 0, keepdims=True)
    return (path_update, new_momentum)


def solution(mesh):
    return jax.shard_map(
        local,
        mesh=mesh,
        in_specs=(P("path", "shard", None), P(None, "shard", "path"), P()),
        out_specs=(P("path", "shard", None), P(None, "shard", "path")),
        check_vma=False,
    )
```

profile of v0, /device:TPU:0, one launch (start us, length us, event | category | flops | bytes accessed | tf_op | source)
XLA Modules:
  0.0 145.2 jit_solution(7055501070345371449)
XLA Ops:
  7.2 4.3 %copy.8 = bf16[1,16,4096]{1,0,2:T(2,128)(2,1)S(1)} copy(bf16[1,16,4096]{2,1,0:T(8,128)(2,1)} %param.3) | data formatting | bytes 262144 | tf_op args[0]
  11.5 0.5 broadcast.26
  12.0 0.0 copy-start.1
  12.0 22.4 %reduce = bf16[4096,16]{1,0:T(8,128)(2,1)S(1)} reduce(bf16[4096,1,16]{2,1,0:T(2,128)(2,1)S(1)} %bitcast.25, bf16[]{:T(256)} %broadcast.26), dimensions={1}, to_apply=%bitcast.15.reduce_sub_computation | reduce | bytes 262146
  34.4 1.8 %reshape.8 = bf16[16,2,2048]{2,1,0:T(2,128)(2,1)} reshape(bf16[4096,16]{1,0:T(8,128)(2,1)S(1)} %reduce) | data formatting | bytes 262144
  36.2 7.4 %all-to-all-start = ((bf16[16,2,2048]{2,1,0:T(2,128)(2,1)}), bf16[16,2,2048]{2,1,0:T(2,128)(2,1)S(1)}, u32[]{:S(2)}, u32[]{:S(2)}) async-start(bf16[16,2,2048]{2,1,0:T(2,128)(2,1)} %reshape.8), calls=%async_computation | async-start | bytes 262144 | tf_op jit(solution)/shard_map/all_to_all | solution.py:21
  43.6 0.0 all-gather.2.cloned.1.call-start
  43.6 0.0 copy-done.1
  43.6 0.1 convert_reduce_fusion
  43.8 7.7 %all-to-all-done = bf16[16,2,2048]{2,1,0:T(2,128)(2,1)S(1)} async-done(((bf16[16,2,2048]{2,1,0:T(2,128)(2,1)}), bf16[16,2,2048]{2,1,0:T(2,128)(2,1)S(1)}, u32[]{:S(2)}, u32[]{:S(2)}) %all-to-all-start) | async-done | bytes 131104 | tf_op jit(solution)/shard_map/all_to_all | solution.py:21
  51.5 1.8 %reshape.9 = bf16[4096,1,16]{2,1,0:T(2,128)(2,1)S(1)} reshape(bf16[16,2,2048]{2,1,0:T(2,128)(2,1)S(1)} %all-to-all-done) | data formatting | bytes 262144
  53.3 0.0 copy-start
  53.3 2.0 %copy.9 = bf16[1,16,4096]{2,1,0:T(8,128)(2,1)S(1)} copy(bf16[1,16,4096]{1,0,2:T(2,128)(2,1)S(1)} %bitcast.26) | data formatting | bytes 262144 | tf_op jit(solution)/shard_map/all_to_all | solution.py:21
  55.3 0.3 multiply_reduce_fusion
  55.6 37.5 %psum.7 = f32[16]{0:T(128)S(1)} all-reduce(f32[16]{0:T(128)S(1)} %get-tuple-element.8), channel_id=1, replica_groups=mesh['path'=16,'shard'=2] {'path','shard'}, use_global_device_ids=true, to_apply=%region_2.3 | all-reduce | flops 16 | bytes 128 | tf_op jit(solution)/shard_map/psum | solution.py:30
  93.1 0.0 copy-done
  93.1 0.9 fusion
  94.0 0.0 all-gather.2.cloned.1.call-update
  94.0 0.6 dynamic_slice.8
  96.5 0.9 copy.12
  97.4 38.6 %all-gather.2.cloned.1.call-done = bf16[16,16,4096]{2,0,1:T(8,128)(2,1)} async-done(((bf16[16,16,256]{2,0,1:T(8,128)(2,1)}), bf16[16,16,4096]{2,0,1:T(8,128)(2,1)}) %all-gather.2.cloned.1.call-update) | async-done | bytes 2097168 | tf_op jit(solution)/shard_map/all_gather | solution.py:36
  136.0 1.5 %constant_dynamic-slice_fusion = bf16[1,16,4096]{2,0,1:T(2,128)(2,1)S(1)} fusion(bf16[16,16,4096]{2,0,1:T(8,128)(2,1)} %all-gather.2.cloned.1.call-done, s32[]{:T(128)S(6)} %select_n.9), kind=kLoop, calls=%fused_computation.12 | loop fusion | bytes 262148 | tf_op jit(solution)/shard_map/jit(dynamic_index_in_dim)/dynamic_slice | solution.py:37
  137.5 0.8 copy.11
  (2 shorter events, 0.0 us)
Async XLA Ops:
  12.0 31.6 %copy-start.1 = (s32[16]{0:T(128)S(1)}, s32[16]{0:T(128)}, u32[]{:S(2)}) copy-start(s32[16]{0:T(128)} %param.5) | copy-start | bytes 196
  36.2 15.3 %all-to-all-start = ((bf16[16,2,2048]{2,1,0:T(2,128)(2,1)}), bf16[16,2,2048]{2,1,0:T(2,128)(2,1)S(1)}, u32[]{:S(2)}, u32[]{:S(2)}) async-start(bf16[16,2,2048]{2,1,0:T(2,128)(2,1)} %reshape.8), calls=%async_computation | async-start | bytes 262144 | tf_op jit(solution)/shard_map/all_to_all | solution.py:21
  43.6 92.4 %all-gather.2.cloned.1.call-start = ((), (), s32[]{:S(2)}) async-start(), calls=%async_computation.1 | async-start | bytes 2228224 | tf_op jit(solution)/shard_map/all_gather | solution.py:36
  53.3 39.8 %copy-start = (f32[16,16,256]{2,1,0:T(8,128)S(1)}, f32[16,16,256]{2,1,0:T(8,128)}, u32[]{:S(2)}) copy-start(f32[16,16,256]{2,1,0:T(8,128)} %param.4) | copy-start | bytes 786436
Sparse Core Ops, SparseCore 0:
  94.1 41.7 all-gather.1
where the time goes:
time: 146 us; the launch traced here: 145 us
  waiting for transfers between devices  46.3 us (32%)
  blocking collectives  37.5 us (26%)
  other arithmetic  23.4 us (16%)
  between operations  16 us (11%)
  local copies, waits for them, and re-layouts  14.2 us (10%)
  starting transfers between devices  7.43 us (5%)
    all_gather x1, waiting for transfers between devices, local(): gathered = lax.all_gather(outer_step, 'path', axis=2, tiled=True)  38.6 us
    psum x1, blocking collectives, local(): norm_squares = lax.psum(local_squares, ('path', 'shard'))  37.5 us
    unnamed x1, other arithmetic  22.4 us
    unnamed x11, local copies, waits for them, and re-layouts  10.1 us
    all_to_all x1, waiting for transfers between devices, local(): lax.all_to_all(deltas, 'path', split_axis=2, concat_axis=0, tiled=True)  7.73 us
    all_to_all x1, starting transfers between devices, local(): lax.all_to_all(deltas, 'path', split_axis=2, concat_axis=0, tiled=True)  7.39 us
  transfers between devices with their start and end apart: 2, of which 2 were waited for; matrix products, arithmetic and copies ran while one was open for 1% of the time, Pallas kernels for 0%

commit v1 on v0

--- a/solution.py
+++ b/solution.py
@@ -33,7 +33,9 @@
     clipped = outer_grad * shrink[:, None, None]
     new_momentum = momentum_rate * momentum + clipped
     outer_step = (outer_rate * (clipped + momentum_rate * new_momentum)).astype(jnp.bfloat16)
-    gathered = lax.all_gather(outer_step, "path", axis=2, tiled=True)
+    gathered = jnp.concatenate(
+        lax.all_to_all(jnp.stack([outer_step] * lax.axis_size("path")), "path", 0, 0), axis=2
+    )
     path_update = lax.dynamic_index_in_dim(gathered, own_module, 0, keepdims=True)
     return (path_update, new_momentum)
 

time: 146 us -> 142 us (0.973)
  the two profiles are of different devices: /device:TPU:0 before, /device:TPU:15 now
where the time goes in v1:
time: 142 us; the launch traced here: 141 us
  waiting for transfers between devices  49.1 us (35%)
  blocking collectives  39.3 us (28%)
  other arithmetic  22.8 us (16%)
  local copies, waits for them, and re-layouts  14.4 us (10%)
  starting transfers between devices  12.8 us (9%)
  between operations  2.65 us (2%)
    all_to_all x1, waiting for transfers between devices, local(): lax.all_to_all(jnp.stack([outer_step] * lax.axis_size('path')), 'path', 0...  44 us
    psum x1, blocking collectives, local(): norm_squares = lax.psum(local_squares, ('path', 'shard'))  39.3 us
    unnamed x1, other arithmetic  22.4 us
    unnamed x10, local copies, waits for them, and re-layouts  9.29 us
    all_to_all x1, starting transfers between devices, local(): lax.all_to_all(deltas, 'path', split_axis=2, concat_axis=0, tiled=True)  6.52 us
    all_to_all x1, starting transfers between devices, local(): lax.all_to_all(jnp.stack([outer_step] * lax.axis_size('path')), 'path', 0...  6.33 us
    all_to_all x1, waiting for transfers between devices, local(): lax.all_to_all(deltas, 'path', split_axis=2, concat_axis=0, tiled=True)  5.05 us
  transfers between devices with their start and end apart: 2, of which 2 were waited for; matrix products, arithmetic and copies ran while one was open for 1% of the time, Pallas kernels for 0%

profile of v1, /device:TPU:15, one launch (start us, length us, event | category | flops | bytes accessed | tf_op | source)
XLA Modules:
  0.0 141.3 jit_solution(11816285266608062329)
XLA Ops:
  0.6 4.3 %copy.13 = bf16[1,16,4096]{1,0,2:T(2,128)(2,1)S(1)} copy(bf16[1,16,4096]{2,1,0:T(8,128)(2,1)} %param.3) | data formatting | bytes 262144 | tf_op args[0]
  5.0 0.5 broadcast.28
  5.5 0.0 copy-start.1
  5.5 22.4 %reduce = bf16[4096,16]{1,0:T(8,128)(2,1)S(1)} reduce(bf16[4096,1,16]{2,1,0:T(2,128)(2,1)S(1)} %bitcast.29, bf16[]{:T(256)} %broadcast.28), dimensions={1}, to_apply=%bitcast.18.reduce_sub_computation | reduce | bytes 262146
  27.9 1.8 %reshape.18 = bf16[16,2,2048]{2,1,0:T(2,128)(2,1)} reshape(bf16[4096,16]{1,0:T(8,128)(2,1)S(1)} %reduce) | data formatting | bytes 262144
  29.7 6.5 %all-to-all-start = ((bf16[16,2,2048]{2,1,0:T(2,128)(2,1)}), bf16[16,2,2048]{2,1,0:T(2,128)(2,1)S(1)}, u32[]{:S(2)}, u32[]{:S(2)}) async-start(bf16[16,2,2048]{2,1,0:T(2,128)(2,1)} %reshape.18), calls=%async_computation | async-start | bytes 262144 | tf_op jit(solution)/shard_map/all_to_all | solution.py:21
  36.2 0.0 copy-done.1
  36.2 0.1 convert_reduce_fusion
  36.3 5.0 %all-to-all-done = bf16[16,2,2048]{2,1,0:T(2,128)(2,1)S(1)} async-done(((bf16[16,2,2048]{2,1,0:T(2,128)(2,1)}), bf16[16,2,2048]{2,1,0:T(2,128)(2,1)S(1)}, u32[]{:S(2)}, u32[]{:S(2)}) %all-to-all-start) | async-done | bytes 131104 | tf_op jit(solution)/shard_map/all_to_all | solution.py:21
  41.3 1.8 %reshape.19 = bf16[4096,1,16]{2,1,0:T(2,128)(2,1)S(1)} reshape(bf16[16,2,2048]{2,1,0:T(2,128)(2,1)S(1)} %all-to-all-done) | data formatting | bytes 262144
  43.2 0.0 copy-start
  43.2 2.0 %copy.14 = bf16[1,16,4096]{2,1,0:T(8,128)(2,1)S(1)} copy(bf16[1,16,4096]{1,0,2:T(2,128)(2,1)S(1)} %bitcast.30) | data formatting | bytes 262144 | tf_op jit(solution)/shard_map/all_to_all | solution.py:21
  45.2 0.3 multiply_reduce_fusion
  45.5 39.3 %psum.7 = f32[16]{0:T(128)S(1)} all-reduce(f32[16]{0:T(128)S(1)} %get-tuple-element.10), channel_id=1, replica_groups=mesh['path'=16,'shard'=2] {'path','shard'}, use_global_device_ids=true, to_apply=%region_2.3 | all-reduce | flops 16 | bytes 128 | tf_op jit(solution)/shard_map/psum | solution.py:30
  84.8 0.0 copy-done
  84.8 0.2 fusion
  85.1 1.6 %stack.2 = bf16[16,16,16,256]{3,2,1,0:T(8,128)(2,1)} broadcast(bf16[16,16,256]{2,1,0:T(8,128)(2,1)S(1)} %copy.16), dimensions={1,2,3} | broadcast | bytes 2228224 | tf_op jit(solution)/shard_map/stack | solution.py:37
  86.6 6.3 %all-to-all-start.1 = ((bf16[16,16,16,256]{3,2,1,0:T(8,128)(2,1)}), bf16[16,16,16,256]{3,2,1,0:T(8,128)(2,1)S(1)}, u32[]{:S(2)}, u32[]{:S(2)}) async-start(bf16[16,16,16,256]{3,2,1,0:T(8,128)(2,1)} %stack.2), calls=%async_computation.1 | async-start | bytes 4194304 | tf_op jit(solution)/shard_map/all_to_all | solution.py:37
  92.9 0.6 dynamic_slice.8
  95.5 0.9 copy.18
  96.3 44.0 %all-to-all-done.1 = bf16[16,16,16,256]{3,2,1,0:T(8,128)(2,1)S(1)} async-done(((bf16[16,16,16,256]{3,2,1,0:T(8,128)(2,1)}), bf16[16,16,16,256]{3,2,1,0:T(8,128)(2,1)S(1)}, u32[]{:S(2)}, u32[]{:S(2)}) %all-to-all-start.1) | async-done | bytes 2097184 | tf_op jit(solution)/shard_map/all_to_all | solution.py:37
  140.4 0.2 copy.19
  140.6 0.7 constant_dynamic-slice_fusion
  (3 shorter events, 0.1 us)
Async XLA Ops:
  5.5 30.7 %copy-start.1 = (s32[16]{0:T(128)S(1)}, s32[16]{0:T(128)}, u32[]{:S(2)}) copy-start(s32[16]{0:T(128)} %param.5) | copy-start | bytes 196
  29.7 11.7 %all-to-all-start = ((bf16[16,2,2048]{2,1,0:T(2,128)(2,1)}), bf16[16,2,2048]{2,1,0:T(2,128)(2,1)S(1)}, u32[]{:S(2)}, u32[]{:S(2)}) async-start(bf16[16,2,2048]{2,1,0:T(2,128)(2,1)} %reshape.18), calls=%async_computation | async-start | bytes 262144 | tf_op jit(solution)/shard_map/all_to_all | solution.py:21
  43.2 41.6 %copy-start = (f32[16,16,256]{2,1,0:T(8,128)S(1)}, f32[16,16,256]{2,1,0:T(8,128)}, u32[]{:S(2)}) copy-start(f32[16,16,256]{2,1,0:T(8,128)} %param.4) | copy-start | bytes 786436
  86.6 53.7 %all-to-all-start.1 = ((bf16[16,16,16,256]{3,2,1,0:T(8,128)(2,1)}), bf16[16,16,16,256]{3,2,1,0:T(8,128)(2,1)S(1)}, u32[]{:S(2)}, u32[]{:S(2)}) async-start(bf16[16,16,16,256]{3,2,1,0:T(8,128)(2,1)} %stack.2), calls=%async_computation.1 | async-start | bytes 4194304 | tf_op jit(solution)/shard_map/all_to_all | solution.py:37
